TPU v7x, 32 devices: a whole 2x2x4 slice. The times are simulated.
32 devices in a mesh: aa: 2 (over y), ba: 4 (over z), col: 4 (over x, core).
Axes of the slice: x: 2, y: 2, z: 4, core: 2. Of those that a mesh axis runs over, the one named last changes fastest.
Arguments:
- amplitudes: bfloat16 [384, 384, 384], P('aa', 'ba', 'col'), as said below
- factors: bfloat16 [4, 384, 384], replicated, may hold values from -0.15625 to 0.15625
- energies: float32 [384], replicated, may hold values from 0.3 to 1.5
Outputs:
- sigma: bfloat16 [384, 384, 384], P('aa', 'ba', 'col')
Inputs may be any that keep to these rules, and one draw needn't show every extreme that they name: amplitudes is antisymmetric: exchanging any two of its three indices changes its sign.
All inputs are finite; a program needn't handle non-finite values.
Results may differ from a plain program's by a relative error of at most 0.0065.
Values may be sent and summed in bfloat16 or wider, within the bound.
A program may use at most 320 MiB of HBM per device.

v0:
```python
import functools

import jax
import jax.numpy as jnp
from jax import lax
from jax.experimental import pallas as pl
from jax.sharding import PartitionSpec as P


def on_device(amplitudes, factors, energies):
    width_a, width_b, width_c = amplitudes.shape
    fitting = factors.shape[0]
    merged = width_b * width_c
    index_a = lax.axis_index("aa")
    index_b = lax.axis_index("ba")
    index_c = lax.axis_index("col")
    rows_a = lax.dynamic_slice_in_dim(factors, index_a * width_a, width_a, 1)
    rows_b = lax.dynamic_slice_in_dim(factors, index_b * width_b, width_b, 1)
    rows_c = lax.dynamic_slice_in_dim(factors, index_c * width_c, width_c, 1)
    energy_a = lax.dynamic_slice_in_dim(energies, index_a * width_a, width_a, 0)
    energy_b = lax.dynamic_slice_in_dim(energies, index_b * width_b, width_b, 0)
    energy_c = lax.dynamic_slice_in_dim(energies, index_c * width_c, width_c, 0)

    def close_c(portion):
        term = jnp.einsum("pabf,pcf->abc", portion, rows_c, preferred_element_type=jnp.float32)
        return term.reshape(width_a, merged)

    shape_x = (fitting, width_a, width_b, width_c)
    shape_w = (width_a, width_b, width_c)
    columns = rows_a
    term = jnp.einsum(
        "pae,ebc->pabc",
        columns,
        lax.all_gather(amplitudes, "aa", axis=0, tiled=True),
        preferred_element_type=jnp.float32,
    )
    along_a = term.reshape(fitting, width_a, merged).astype(jnp.bfloat16).reshape(shape_x)
    columns = rows_b
    term = jnp.einsum(
        "pbe,aec->pabc",
        columns,
        lax.all_gather(amplitudes, "ba", axis=1, tiled=True),
        preferred_element_type=jnp.float32,
    )
    along_b = term.reshape(fitting, width_a, merged).astype(jnp.bfloat16).reshape(shape_x)
    ladder_ac = close_c(lax.all_gather(along_a, "col", axis=3, tiled=True))
    ladder_bc = close_c(lax.all_gather(along_b, "col", axis=3, tiled=True))
    block_b = lax.dynamic_slice_in_dim(factors, index_b * width_b, width_b, 2)
    terms_ab = jnp.einsum("pafc,pbf->abc", along_a, block_b, preferred_element_type=jnp.float32)
    ladder_ab = (
        lax.psum_scatter(terms_ab.astype(jnp.bfloat16), "ba", scatter_dimension=1, tiled=True)
        .astype(jnp.float32)
        .reshape(width_a, merged)
    )
    shifts = energy_a[:, None, None] + energy_b[None, :, None] + energy_c[None, None, :]
    ladders = (ladder_ab + ladder_bc + ladder_ac).reshape(shape_w)
    result = 2.0 * ladders + shifts * amplitudes.astype(jnp.float32)
    return result.astype(jnp.bfloat16)


def ladder_kernel(fitting, stacked_ref, slab_ref, out_ref):
    size = slab_ref.shape[1]
    once = jnp.dot(stacked_ref[...], slab_ref[0], preferred_element_type=jnp.float32).astype(jnp.bfloat16)
    total = None
    for p in range(fitting):
        rows = slice(p * size, (p + 1) * size)
        term = lax.dot_general(
            once[rows], stacked_ref[rows, :], (((1,), (1,)), ((), ())), preferred_element_type=jnp.float32
        )
        total = term if total is None else total + term
    out_ref[0] = total.astype(out_ref.dtype)


def ladder_of_slabs(slabs, stacked, fitting):
    count, size, _ = slabs.shape
    block = pl.BlockSpec((1, size, size), lambda i: (i, 0, 0))
    return pl.pallas_call(
        functools.partial(ladder_kernel, fitting),
        grid=(count,),
        in_specs=[pl.BlockSpec(stacked.shape, lambda i: (0, 0)), block],
        out_specs=block,
        out_shape=jax.ShapeDtypeStruct(slabs.shape, jnp.bfloat16),
        cost_estimate=pl.CostEstimate(
            flops=4 * count * fitting * size**3, bytes_accessed=4 * slabs.size, transcendentals=0
        ),
    )(stacked, slabs)


def two_index_ladder(portion, stacked, fitting, axes, counts):
    outer, rows, columns = portion.shape
    n_rows, n_columns = counts
    each = outer // (n_rows * n_columns)
    slabs = lax.all_to_all(portion, axes, 0, 0, tiled=True)
    slabs = slabs.reshape(n_rows, n_columns, each, rows, columns).transpose(2, 0, 3, 1, 4)
    slabs = slabs.reshape(each, n_rows * rows, n_columns * columns)
    term = ladder_of_slabs(slabs, stacked, fitting)
    term = term.reshape(each, n_rows, rows, n_columns, columns).transpose(1, 3, 0, 2, 4)
    return lax.all_to_all(term.reshape(outer, rows, columns), axes, 0, 0, tiled=True)


def by_slabs(sizes, amplitudes, factors, energies):
    width_a, width_b, width_c = amplitudes.shape
    fitting, size, _ = factors.shape
    n_a, n_b, n_c = sizes
    stacked = factors.reshape(fitting * size, size)
    energy_a = lax.dynamic_slice_in_dim(energies, lax.axis_index("aa") * width_a, width_a, 0)
    energy_b = lax.dynamic_slice_in_dim(energies, lax.axis_index("ba") * width_b, width_b, 0)
    energy_c = lax.dynamic_slice_in_dim(energies, lax.axis_index("col") * width_c, width_c, 0)
    ab = two_index_ladder(amplitudes.transpose(2, 0, 1), stacked, fitting, ("aa", "ba"), (n_a, n_b))
    ac = two_index_ladder(amplitudes.transpose(1, 0, 2), stacked, fitting, ("aa", "col"), (n_a, n_c))
    bc = two_index_ladder(amplitudes, stacked, fitting, ("ba", "col"), (n_b, n_c))
    ladders = (
        ab.transpose(1, 2, 0).astype(jnp.float32)
        + bc.astype(jnp.float32)
        + ac.transpose(1, 0, 2).astype(jnp.float32)
    )
    shifts = energy_a[:, None, None] + energy_b[None, :, None] + energy_c[None, None, :]
    return (2.0 * ladders + shifts * amplitudes.astype(jnp.float32)).astype(jnp.bfloat16)


def solution(mesh):
    sizes = tuple(mesh.shape[name] for name in ("aa", "ba", "col"))

    def body(amplitudes, factors, energies):
        n_a, n_b, n_c = sizes
        width_a, width_b, width_c = amplitudes.shape
        if width_a % (n_b * n_c) or width_b % (n_a * n_c) or width_c % (n_a * n_b):
            return on_device(amplitudes, factors, energies)
        return by_slabs(sizes, amplitudes, factors, energies)

    return jax.shard_map(
        body,
        mesh=mesh,
        in_specs=(P("aa", "ba", "col"), P(), P()),
        out_specs=P("aa", "ba", "col"),
        check_vma=False,
    )
```

profile of v0, /device:TPU:11, one launch (start us, length us, event | category | flops | bytes accessed | tf_op | source)
XLA Modules:
  0.0 630.8 jit_solution(12351379122587085646)
XLA Ops:
  0.0 4.2 copy.52
  4.2 57.3 %all_to_all.30 = bf16[96,192,96]{2,1,0:T(8,128)(2,1)S(1)} all-to-all(bf16[96,192,96]{2,1,0:T(8,128)(2,1)S(1)} %bitcast.42), channel_id=1, replica_groups=mesh['aa'=2,'ba'=4,'col'=4] {'aa','col'}, dimensions={0} | all-to-all | bytes 7077888 | tf_op jit(solution)/shard_map/all_to_all | solution.py:93
  61.5 6.4 %copy.41 = bf16[12,2,192,4,96]{4,3,2,1,0:T(4,128)(2,1)} copy(bf16[12,2,192,4,96]{4,2,0,3,1:T(8,128)(2,1)S(1)} %bitcast.41) | data formatting | bytes 7077888 | tf_op jit(solution)/shard_map/transpose | solution.py:94
  67.9 8.2 %reshape.82.slab_ref = bf16[12,384,384]{2,1,0:T(8,128)(2,1)} reshape(bf16[12,2,192,4,96]{4,3,2,1,0:T(4,128)(2,1)} %copy.41) | data formatting | bytes 7077888 | tf_op jit(solution)/shard_map/reshape | solution.py:95
  76.0 21.6 %shard_map.39 = bf16[12,384,384]{2,1,0:T(8,128)(2,1)} custom-call(bf16[1536,384]{1,0:T(8,128)(2,1)} %bitcast.44, bf16[12,384,384]{2,1,0:T(8,128)(2,1)} %reshape.82.slab_ref), custom_call_target="tpu_custom_call" | custom-call | flops 10871635968 | bytes 7077888 | tf_op jit(solution)/shard_map/pallas_call | solution.py:77
  97.6 9.6 %reshape.83 = bf16[12,2,192,4,96]{4,3,2,1,0:T(4,128)(2,1)} reshape(bf16[12,384,384]{2,1,0:T(8,128)(2,1)} %shard_map.39) | data formatting | bytes 7077888 | tf_op jit(solution)/shard_map/reshape | solution.py:97
  107.2 9.7 %copy.48 = bf16[12,2,192,4,96]{2,4,0,3,1:T(8,128)(2,1)} copy(bf16[12,2,192,4,96]{4,3,2,1,0:T(4,128)(2,1)} %reshape.83) | data formatting | bytes 7077888 | tf_op jit(solution)/shard_map/reshape | solution.py:98
  116.9 6.2 all-to-all-start.5
  123.1 9.1 %copy.33 = bf16[192,96,96]{1,0,2:T(8,128)(2,1)} copy(bf16[192,96,96]{2,1,0:T(8,128)(2,1)} %param.3) | data formatting | bytes 7077888 | tf_op args[0]
  132.2 44.1 %all-to-all-done.5 = bf16[96,192,96]{1,2,0:T(8,128)(2,1)} async-done(((bf16[96,192,96]{1,2,0:T(8,128)(2,1)}), bf16[96,192,96]{1,2,0:T(8,128)(2,1)}, u32[]{:S(2)}, u32[]{:S(2)}) %all-to-all-start.5) | async-done | bytes 3538976 | tf_op jit(solution)/shard_map/all_to_all | solution.py:98
  176.3 106.6 %all_to_all.31 = bf16[96,192,96]{2,1,0:T(8,128)(2,1)} all-to-all(bf16[96,192,96]{2,1,0:T(8,128)(2,1)} %bitcast.36), channel_id=1, replica_groups=mesh['aa'=2,'ba'=4,'col'=4] {'aa','ba'}, dimensions={0} | all-to-all | bytes 7077888 | tf_op jit(solution)/shard_map/all_to_all | solution.py:93
  282.9 7.5 %all-to-all-start.2 = ((bf16[192,96,96]{2,1,0:T(8,128)(2,1)}), bf16[192,96,96]{2,1,0:T(8,128)(2,1)}, u32[]{:S(2)}, u32[]{:S(2)}) async-start(bf16[192,96,96]{2,1,0:T(8,128)(2,1)} %param.3), calls=%async_computation.2 | async-start | bytes 9437184 | tf_op jit(solution)/shard_map/all_to_all | solution.py:93
  290.4 8.8 %copy.34 = bf16[12,2,192,4,96]{4,3,2,1,0:T(4,128)(2,1)} copy(bf16[12,2,192,4,96]{4,2,0,3,1:T(8,128)(2,1)} %bitcast.40) | data formatting | bytes 7077888 | tf_op jit(solution)/shard_map/transpose | solution.py:94
  299.2 8.2 %reshape.74.slab_ref = bf16[12,384,384]{2,1,0:T(8,128)(2,1)} reshape(bf16[12,2,192,4,96]{4,3,2,1,0:T(4,128)(2,1)} %copy.34) | data formatting | bytes 7077888 | tf_op jit(solution)/shard_map/reshape | solution.py:95
  307.4 21.6 %shard_map.37 = bf16[12,384,384]{2,1,0:T(8,128)(2,1)} custom-call(bf16[1536,384]{1,0:T(8,128)(2,1)} %bitcast.45, bf16[12,384,384]{2,1,0:T(8,128)(2,1)} %reshape.74.slab_ref), custom_call_target="tpu_custom_call" | custom-call | flops 10871635968 | bytes 7077888 | tf_op jit(solution)/shard_map/pallas_call | solution.py:77
  329.0 9.6 %reshape.75 = bf16[12,2,192,4,96]{4,3,2,1,0:T(4,128)(2,1)} reshape(bf16[12,384,384]{2,1,0:T(8,128)(2,1)} %shard_map.37) | data formatting | bytes 7077888 | tf_op jit(solution)/shard_map/reshape | solution.py:97
  338.6 5.7 copy.35
  344.3 49.8 %all-to-all-done.2 = bf16[192,96,96]{2,1,0:T(8,128)(2,1)} async-done(((bf16[192,96,96]{2,1,0:T(8,128)(2,1)}), bf16[192,96,96]{2,1,0:T(8,128)(2,1)}, u32[]{:S(2)}, u32[]{:S(2)}) %all-to-all-start.2) | async-done | bytes 3538976 | tf_op jit(solution)/shard_map/all_to_all | solution.py:93
  394.1 4.8 all-to-all-start.1
  398.9 8.2 %copy.53 = bf16[4,4,12,96,96]{4,1,3,0,2:T(4,128)(2,1)} copy(bf16[4,4,12,96,96]{4,3,2,1,0:T(8,128)(2,1)} %bitcast.7) | data formatting | bytes 7077888 | tf_op jit(solution)/shard_map/reshape | solution.py:94
  407.1 8.2 %reshape.78.slab_ref = bf16[12,384,384]{2,1,0:T(8,128)(2,1)} reshape(bf16[12,4,96,4,96]{4,3,2,1,0:T(4,128)(2,1)} %bitcast.43) | data formatting | bytes 7077888 | tf_op jit(solution)/shard_map/reshape | solution.py:95
  415.2 21.6 %shard_map.38 = bf16[12,384,384]{2,1,0:T(8,128)(2,1)} custom-call(bf16[1536,384]{1,0:T(8,128)(2,1)} %bitcast.46, bf16[12,384,384]{2,1,0:T(8,128)(2,1)} %reshape.78.slab_ref), custom_call_target="tpu_custom_call" | custom-call | flops 10871635968 | bytes 7077888 | tf_op jit(solution)/shard_map/pallas_call | solution.py:77
  436.8 9.6 %reshape.79 = bf16[12,4,96,4,96]{4,3,2,1,0:T(4,128)(2,1)} reshape(bf16[12,384,384]{2,1,0:T(8,128)(2,1)} %shard_map.38) | data formatting | bytes 7077888 | tf_op jit(solution)/shard_map/reshape | solution.py:97
  446.4 9.6 %copy.47 = bf16[12,4,96,4,96]{2,4,0,3,1:T(8,128)(2,1)} copy(bf16[12,4,96,4,96]{4,3,2,1,0:T(4,128)(2,1)} %reshape.79) | data formatting | bytes 7077888 | tf_op jit(solution)/shard_map/reshape | solution.py:98
  456.0 43.4 %all-to-all-done.1 = bf16[96,192,96]{2,1,0:T(8,128)(2,1)} async-done(((bf16[96,192,96]{2,1,0:T(8,128)(2,1)}), bf16[96,192,96]{2,1,0:T(8,128)(2,1)}, u32[]{:S(2)}, u32[]{:S(2)}) %all-to-all-start.1) | async-done | bytes 3538976 | tf_op jit(solution)/shard_map/all_to_all | solution.py:98
  499.4 8.8 %all-to-all-start.3 = ((bf16[192,96,96]{1,2,0:T(8,128)(2,1)}), bf16[192,96,96]{1,2,0:T(8,128)(2,1)}, u32[]{:S(2)}, u32[]{:S(2)}) async-start(bf16[192,96,96]{1,2,0:T(8,128)(2,1)} %bitcast.37), calls=%async_computation.3 | async-start | bytes 9437184 | tf_op jit(solution)/shard_map/all_to_all | solution.py:98
  508.2 0.1 dynamic_slice.9
  508.4 0.1 broadcast_add_fusion
  508.5 8.2 %copy.44 = bf16[96,192,96]{0,1,2:T(8,128)(2,1)} copy(bf16[96,192,96]{1,2,0:T(8,128)(2,1)} %all-to-all-done.5) | data formatting | bytes 7077888 | tf_op jit(solution)/shard_map/all_to_all | solution.py:98
  516.6 95.3 %all-to-all-done.3 = bf16[192,96,96]{1,2,0:T(8,128)(2,1)} async-done(((bf16[192,96,96]{1,2,0:T(8,128)(2,1)}), bf16[192,96,96]{1,2,0:T(8,128)(2,1)}, u32[]{:S(2)}, u32[]{:S(2)}) %all-to-all-start.3) | async-done | bytes 3538976 | tf_op jit(solution)/shard_map/all_to_all | solution.py:98
  611.9 10.8 %fusion.2 = bf16[192,96,96]{1,0,2:T(8,128)(2,1)} fusion(bf16[96,192,96]{0,1,2:T(8,128)(2,1)} %copy.44, bf16[96,192,96]{2,1,0:T(8,128)(2,1)} %all-to-all-done.1, bf16[192,96,96]{1,0,2:T(8,128)(2,1)} %copy.33, bf16[192,96,96]{1,2,0:T(8,128)(2,1)} %all-to-all-done.3, f32[96]{0:T(128)S(1)} %get-tuple-element.6, f32[192,96]{1,0:T(8,128)S(1)} %broadcast_add_fusion), kind=kLoop, calls=%fused_computation.3 | loop fusion | flops 19464192 | bytes 17768832 | tf_op jit(solution)/shard_map/convert_element_type | solution.py:118
  622.7 8.1 %copy.46 = bf16[192,96,96]{2,1,0:T(8,128)(2,1)} copy(bf16[192,96,96]{1,0,2:T(8,128)(2,1)} %fusion.2) | data formatting | bytes 7077888 | tf_op jit(solution)/shard_map/convert_element_type | solution.py:118
  (3 shorter events, 0.1 us)
Async XLA Ops:
  116.9 59.4 %all-to-all-start.5 = ((bf16[96,192,96]{1,2,0:T(8,128)(2,1)}), bf16[96,192,96]{1,2,0:T(8,128)(2,1)}, u32[]{:S(2)}, u32[]{:S(2)}) async-start(bf16[96,192,96]{1,2,0:T(8,128)(2,1)} %bitcast.39), calls=%async_computation.5 | async-start | bytes 9437184 | tf_op jit(solution)/shard_map/all_to_all | solution.py:98
  282.9 111.2 %all-to-all-start.2 = ((bf16[192,96,96]{2,1,0:T(8,128)(2,1)}), bf16[192,96,96]{2,1,0:T(8,128)(2,1)}, u32[]{:S(2)}, u32[]{:S(2)}) async-start(bf16[192,96,96]{2,1,0:T(8,128)(2,1)} %param.3), calls=%async_computation.2 | async-start | bytes 9437184 | tf_op jit(solution)/shard_map/all_to_all | solution.py:93
  394.1 105.3 %all-to-all-start.1 = ((bf16[96,192,96]{2,1,0:T(8,128)(2,1)}), bf16[96,192,96]{2,1,0:T(8,128)(2,1)}, u32[]{:S(2)}, u32[]{:S(2)}) async-start(bf16[96,192,96]{2,1,0:T(8,128)(2,1)} %bitcast.38), calls=%async_computation.1 | async-start | bytes 9437184 | tf_op jit(solution)/shard_map/all_to_all | solution.py:98
  499.4 8.8 %copy-start = (f32[384]{0:T(512)S(1)}, f32[384]{0:T(512)}, u32[]{:S(2)}) copy-start(f32[384]{0:T(512)} %param.5) | copy-start | bytes 4612
  499.4 112.6 %all-to-all-start.3 = ((bf16[192,96,96]{1,2,0:T(8,128)(2,1)}), bf16[192,96,96]{1,2,0:T(8,128)(2,1)}, u32[]{:S(2)}, u32[]{:S(2)}) async-start(bf16[192,96,96]{1,2,0:T(8,128)(2,1)} %bitcast.37), calls=%async_computation.3 | async-start | bytes 9437184 | tf_op jit(solution)/shard_map/all_to_all | solution.py:98
where the time goes:
time: 633 us; the launch traced here: 631 us
  waiting for transfers between devices  233 us (37%)
  blocking collectives  164 us (26%)
  local copies, waits for them, and re-layouts  131 us (21%)
  Pallas kernels  64.8 us (10%)
  starting transfers between devices  27.3 us (4%)
  other arithmetic  10.8 us (2%)
    all_to_all x3, waiting for transfers between devices, two_index_ladder(): lax.all_to_all(term.reshape(outer, rows, columns), axes, 0, 0, tiled=True)  183 us
    all_to_all x2, blocking collectives, two_index_ladder(): slabs = lax.all_to_all(portion, axes, 0, 0, tiled=True)  164 us
    pallas_call x3, Pallas kernels, ladder_of_slabs(): pl.pallas_call(functools.partial(ladder_kernel, fitting), grid=(count,),...  64.8 us
    all_to_all x1, waiting for transfers between devices, two_index_ladder(): slabs = lax.all_to_all(portion, axes, 0, 0, tiled=True)  49.8 us
    reshape x4, local copies, waits for them, and re-layouts, two_index_ladder(): term.reshape(each, n_rows, rows, n_columns, columns)  34.5 us
    reshape x3, local copies, waits for them, and re-layouts, two_index_ladder(): slabs = slabs.reshape(each, n_rows * rows, n_columns * columns)  24.6 us
    all_to_all x3, starting transfers between devices, two_index_ladder(): lax.all_to_all(term.reshape(outer, rows, columns), axes, 0, 0, tiled=True)  19.8 us
    reshape x2, local copies, waits for them, and re-layouts, two_index_ladder(): term.reshape(outer, rows, columns)  19.3 us
  transfers between devices with their start and end apart: 4, of which 4 were waited for; matrix products, arithmetic and copies ran while one was open for 14% of the time, Pallas kernels for 7%

commit v1 on v0

v1 whole, which is shorter than its diff:
```python
import functools

import jax
import jax.numpy as jnp
from jax import lax
from jax.experimental import pallas as pl
from jax.experimental.pallas import tpu as pltpu
from jax.sharding import PartitionSpec as P


def on_device(amplitudes, factors, energies):
    width_a, width_b, width_c = amplitudes.shape
    fitting = factors.shape[0]
    merged = width_b * width_c
    index_a = lax.axis_index("aa")
    index_b = lax.axis_index("ba")
    index_c = lax.axis_index("col")
    rows_a = lax.dynamic_slice_in_dim(factors, index_a * width_a, width_a, 1)
    rows_b = lax.dynamic_slice_in_dim(factors, index_b * width_b, width_b, 1)
    rows_c = lax.dynamic_slice_in_dim(factors, index_c * width_c, width_c, 1)
    energy_a = lax.dynamic_slice_in_dim(energies, index_a * width_a, width_a, 0)
    energy_b = lax.dynamic_slice_in_dim(energies, index_b * width_b, width_b, 0)
    energy_c = lax.dynamic_slice_in_dim(energies, index_c * width_c, width_c, 0)

    def close_c(portion):
        term = jnp.einsum("pabf,pcf->abc", portion, rows_c, preferred_element_type=jnp.float32)
        return term.reshape(width_a, merged)

    shape_x = (fitting, width_a, width_b, width_c)
    shape_w = (width_a, width_b, width_c)
    columns = rows_a
    term = jnp.einsum(
        "pae,ebc->pabc",
        columns,
        lax.all_gather(amplitudes, "aa", axis=0, tiled=True),
        preferred_element_type=jnp.float32,
    )
    along_a = term.reshape(fitting, width_a, merged).astype(jnp.bfloat16).reshape(shape_x)
    columns = rows_b
    term = jnp.einsum(
        "pbe,aec->pabc",
        columns,
        lax.all_gather(amplitudes, "ba", axis=1, tiled=True),
        preferred_element_type=jnp.float32,
    )
    along_b = term.reshape(fitting, width_a, merged).astype(jnp.bfloat16).reshape(shape_x)
    ladder_ac = close_c(lax.all_gather(along_a, "col", axis=3, tiled=True))
    ladder_bc = close_c(lax.all_gather(along_b, "col", axis=3, tiled=True))
    block_b = lax.dynamic_slice_in_dim(factors, index_b * width_b, width_b, 2)
    terms_ab = jnp.einsum("pafc,pbf->abc", along_a, block_b, preferred_element_type=jnp.float32)
    ladder_ab = (
        lax.psum_scatter(terms_ab.astype(jnp.bfloat16), "ba", scatter_dimension=1, tiled=True)
        .astype(jnp.float32)
        .reshape(width_a, merged)
    )
    shifts = energy_a[:, None, None] + energy_b[None, :, None] + energy_c[None, None, :]
    ladders = (ladder_ab + ladder_bc + ladder_ac).reshape(shape_w)
    result = 2.0 * ladders + shifts * amplitudes.astype(jnp.float32)
    return result.astype(jnp.bfloat16)


LANES = 128


def pack_kernel(rows, amplitudes_ref, out_ref, wide):
    width_a, group, width_c = amplitudes_ref.shape
    wide[:, :width_c] = amplitudes_ref[...].astype(jnp.float32).reshape(width_a * group, width_c)
    for b in range(group):
        block = wide[pl.ds(b, width_a, stride=group), :][:, :width_c]
        out_ref[b] = folded(block, rows).astype(out_ref.dtype)


def folded(block, rows):
    width_a, width_c = block.shape
    spare = LANES - width_c
    rest = block[rows:]
    extra = jnp.concatenate([rest[:, i * spare : (i + 1) * spare] for i in range(width_c // spare)], axis=0)
    return jnp.concatenate([block[:rows], extra], axis=1)


def unfolded(packed, width_a, width_c):
    rows = packed.shape[0]
    spare = LANES - width_c
    left = width_a - rows
    rest = [packed[i * left : (i + 1) * left, width_c:] for i in range(width_c // spare)]
    return jnp.concatenate([packed[:, :width_c], jnp.concatenate(rest, axis=1)], axis=0)


def pack(amplitudes, group, rows):
    width_a, width_b, width_c = amplitudes.shape
    return pl.pallas_call(
        functools.partial(pack_kernel, rows),
        grid=(width_b // group,),
        in_specs=[pl.BlockSpec((width_a, group, width_c), lambda g: (0, g, 0))],
        out_specs=pl.BlockSpec((group, rows, LANES), lambda g: (g, 0, 0)),
        out_shape=jax.ShapeDtypeStruct((width_b, rows, LANES), amplitudes.dtype),
        scratch_shapes=[pltpu.VMEM((width_a * group, LANES), jnp.float32)],
    )(amplitudes)


def ladder_kernel(sizes, portion_ref, stacked_ref, closing_ref, ladder_ref, rows_ref, slab, once, wide):
    n_a, n_c, width_a, width_c, share = sizes
    count = portion_ref.shape[1]
    size = stacked_ref.shape[1]
    fitting = stacked_ref.shape[0] // size
    for s in range(count):
        for i in range(n_a):
            for k in range(n_c):
                block = unfolded(portion_ref[i * n_c + k, s].astype(jnp.float32), width_a, width_c)
                wide[i * width_a : (i + 1) * width_a, k * width_c : (k + 1) * width_c] = block
        slab[:, s * size : (s + 1) * size] = wide[...].astype(slab.dtype)
    for p in range(fitting):
        half = jnp.dot(
            stacked_ref[p * size : (p + 1) * size, :], slab[...], preferred_element_type=jnp.float32
        ).astype(once.dtype)
        for s in range(count):
            once[s * size : (s + 1) * size, p * size : (p + 1) * size] = half[:, s * size : (s + 1) * size]
    for s in range(count):
        wide[...] = jnp.dot(
            once[s * size : (s + 1) * size, :], closing_ref[...], preferred_element_type=jnp.float32
        )
        ladder_ref[s] = wide[...].astype(ladder_ref.dtype)
        for d in range(size // share):
            rows_ref[d, s * share : (s + 1) * share, :] = wide[d * share : (d + 1) * share, :].astype(rows_ref.dtype)


def ladders_of_slabs(sizes, portion, stacked, closing, count):
    n_a, n_c, width_a, width_c, share = sizes
    peers, _, rows, _ = portion.shape
    size = stacked.shape[1]
    devices = size // share
    fitting = stacked.shape[0] // size
    return pl.pallas_call(
        functools.partial(ladder_kernel, sizes),
        grid=(share // count,),
        in_specs=[
            pl.BlockSpec((peers, count, rows, LANES), lambda g: (0, g, 0, 0)),
            pl.BlockSpec(stacked.shape, lambda g: (0, 0)),
            pl.BlockSpec(closing.shape, lambda g: (0, 0)),
        ],
        out_specs=[
            pl.BlockSpec((count, size, size), lambda g: (g, 0, 0)),
            pl.BlockSpec((devices, count * share, size), lambda g: (0, g, 0)),
        ],
        out_shape=[
            jax.ShapeDtypeStruct((share, size, size), portion.dtype),
            jax.ShapeDtypeStruct((devices, share * share, size), portion.dtype),
        ],
        scratch_shapes=[
            pltpu.VMEM((size, count * size), portion.dtype),
            pltpu.VMEM((count * size, fitting * size), portion.dtype),
            pltpu.VMEM((size, size), jnp.float32),
        ],
        cost_estimate=pl.CostEstimate(
            flops=4 * share * fitting * size**3, bytes_accessed=8 * share * size * size, transcendentals=0
        ),
    )(portion, stacked, closing)


def joining_kernel(sizes, ladder_ref, rows_ref, out_ref, wide):
    n_a, n_b, n_c, width_a, width_c, rows = sizes
    share, size, _ = ladder_ref.shape
    chunk = share * share

    @pl.when(pl.program_id(0) == 0)
    def _():
        for j in range(n_b):
            for i in range(n_a):
                for k in range(n_c):
                    at = ((j * n_a + i) * n_c + k) * chunk
                    piece = rows_ref[(i * n_b + j) * n_c + k].astype(jnp.float32)
                    for tile in range(size // LANES):
                        wide[tile, at : at + chunk, :] = piece[:, tile * LANES : (tile + 1) * LANES]

    for b in range(share):
        tiles = [wide[tile, pl.ds(b, size, stride=share), :] for tile in range(size // LANES)]
        crossed = jnp.concatenate(tiles, axis=1)
        total = ladder_ref[b].astype(jnp.float32) + crossed.T - crossed
        for i in range(n_a):
            for k in range(n_c):
                block = total[i * width_a : (i + 1) * width_a, k * width_c : (k + 1) * width_c]
                out_ref[i * n_c + k, b] = folded(block, rows).astype(out_ref.dtype)


def joined(sizes, ladder, crossing):
    n_a, n_b, n_c, width_a, width_c, rows = sizes
    share, size, _ = ladder.shape
    return pl.pallas_call(
        functools.partial(joining_kernel, sizes),
        grid=(1,),
        in_specs=[
            pl.BlockSpec(ladder.shape, lambda g: (0, 0, 0)),
            pl.BlockSpec(crossing.shape, lambda g: (0, 0, 0)),
        ],
        out_specs=pl.BlockSpec((n_a * n_c, share, rows, LANES), lambda g: (0, 0, 0, 0)),
        out_shape=jax.ShapeDtypeStruct((n_a * n_c, share, rows, LANES), ladder.dtype),
        scratch_shapes=[pltpu.VMEM((size // LANES, size * share, LANES), jnp.float32)],
    )(ladder, crossing)


def closing_kernel(total_ref, amplitudes_ref, shift_a_ref, shift_b_ref, shift_c_ref, out_ref, wide):
    width_a, group, width_c = amplitudes_ref.shape
    for b in range(group):
        block = unfolded(total_ref[b].astype(jnp.float32), width_a, width_c)
        block = jnp.concatenate([block, jnp.zeros((width_a, LANES - width_c), jnp.float32)], axis=1)
        wide[pl.ds(b, width_a, stride=group), :] = block
    shifts = shift_a_ref[...] + shift_b_ref[...] + shift_c_ref[...]
    total = wide[:, :width_c].reshape(width_a, group, width_c)
    out_ref[...] = (2.0 * total + shifts * amplitudes_ref[...].astype(jnp.float32)).astype(out_ref.dtype)


def closed(total, amplitudes, energy_a, energy_b, energy_c, group):
    width_a, width_b, width_c = amplitudes.shape
    rows = total.shape[1]
    block = pl.BlockSpec((width_a, group, width_c), lambda g: (0, g, 0))
    return pl.pallas_call(
        closing_kernel,
        grid=(width_b // group,),
        in_specs=[
            pl.BlockSpec((group, rows, LANES), lambda g: (g, 0, 0)),
            block,
            pl.BlockSpec((width_a, 1, 1), lambda g: (0, 0, 0)),
            pl.BlockSpec((1, group, 1), lambda g: (0, g, 0)),
            pl.BlockSpec((1, 1, width_c), lambda g: (0, 0, 0)),
        ],
        out_specs=block,
        out_shape=jax.ShapeDtypeStruct(amplitudes.shape, amplitudes.dtype),
        scratch_shapes=[pltpu.VMEM((width_a * group, LANES), jnp.float32)],
    )(total, amplitudes, energy_a[:, None, None], energy_b[None, :, None], energy_c[None, None, :])


def by_slabs(sizes, amplitudes, factors, energies):
    width_a, width_b, width_c = amplitudes.shape
    fitting, size, _ = factors.shape
    n_a, n_b, n_c = sizes
    peers = n_a * n_c
    share = width_b // peers
    rows = width_a * width_c // LANES
    stacked = factors.reshape(fitting * size, size)
    closing = factors.transpose(0, 2, 1).reshape(fitting * size, size)
    energy_a = lax.dynamic_slice_in_dim(energies, lax.axis_index("aa") * width_a, width_a, 0)
    energy_b = lax.dynamic_slice_in_dim(energies, lax.axis_index("ba") * width_b, width_b, 0)
    energy_c = lax.dynamic_slice_in_dim(energies, lax.axis_index("col") * width_c, width_c, 0)
    packed = pack(amplitudes, 16, rows).reshape(peers, share * rows, LANES)
    portion = lax.all_to_all(packed, ("aa", "col"), 0, 0, tiled=True).reshape(peers, share, rows, LANES)
    ladder, crossing = ladders_of_slabs((n_a, n_c, width_a, width_c, share), portion, stacked, closing, 4)
    crossing = crossing.reshape(n_b, n_a, n_c, share * share, size).transpose(1, 0, 2, 3, 4)
    crossing = crossing.reshape(n_a * n_b * n_c, share * share, size)
    crossing = lax.all_to_all(crossing, ("aa", "ba", "col"), 0, 0, tiled=True)
    total = joined((n_a, n_b, n_c, width_a, width_c, rows), ladder, crossing)
    total = lax.all_to_all(total.reshape(peers, share * rows, LANES), ("aa", "col"), 0, 0, tiled=True)
    return closed(total.reshape(width_b, rows, LANES), amplitudes, energy_a, energy_b, energy_c, 16)


def fits(sizes, shape, size):
    n_a, n_b, n_c = sizes
    width_a, width_b, width_c = shape
    spare = LANES - width_c
    if spare <= 0 or width_c % spare or width_a * width_c % LANES or size % LANES:
        return False
    rows = width_a * width_c // LANES
    share = width_b // (n_a * n_c)
    return (
        rows % 16 == 0
        and (width_a - rows) * (width_c // spare) == rows
        and width_b % (n_a * n_c) == 0
        and share % 4 == 0
        and width_b % 16 == 0
    )


def solution(mesh):
    sizes = tuple(mesh.shape[name] for name in ("aa", "ba", "col"))

    def body(amplitudes, factors, energies):
        if fits(sizes, amplitudes.shape, factors.shape[1]):
            return by_slabs(sizes, amplitudes, factors, energies)
        return on_device(amplitudes, factors, energies)

    return jax.shard_map(
        body,
        mesh=mesh,
        in_specs=(P("aa", "ba", "col"), P(), P()),
        out_specs=P("aa", "ba", "col"),
        check_vma=False,
    )
```

time: 633 us -> 236 us (0.37)
  waiting for transfers between devices: 233 us -> 76.4 us
  local copies, waits for them, and re-layouts: 131 us -> 10.5 us
  blocking collectives: 164 us -> 83.9 us
  starting transfers between devices: 27.3 us -> 9.74 us
  Pallas kernels: 64.8 us -> 51.4 us
  other arithmetic: 10.8 us -> 0 us
    all_to_all x4 -> x2, waiting for transfers between devices: 233 us -> 76.4 us  [the longest x1 38.3 us: by_slabs(): lax.all_to_all(total.reshape(peers, share * rows, LANES), ('aa', 'col'),...]
    reshape x10 -> x1, local copies, waits for them, and re-layouts: 86.5 us -> 2.36 us  [by_slabs(): crossing.reshape(n_b, n_a, n_c, share * share, size)]
    all_to_all x2 -> x1, blocking collectives: 164 us -> 83.9 us  [by_slabs(): crossing = lax.all_to_all(crossing, ('aa', 'ba', 'col'), 0, 0, tiled=True)]
    all_to_all x4 -> x2, starting transfers between devices: 27.3 us -> 9.74 us  [the longest x1 5.21 us: by_slabs(): lax.all_to_all(total.reshape(peers, share * rows, LANES), ('aa', 'col'),...]
    pallas_call x3 -> x4, Pallas kernels: 64.8 us -> 51.4 us  [the longest x1 20.1 us: ladders_of_slabs(): pl.pallas_call(functools.partial(ladder_kernel, sizes), grid=(share // co...]
    transpose x2 -> x1, local copies, waits for them, and re-layouts: 15.2 us -> 2.4 us  [by_slabs(): closing = factors.transpose(0, 2, 1).reshape(fitting * size, size)]
    convert_element_type x1 -> x0, other arithmetic: 10.8 us -> none  [by_slabs(): (2.0 * ladders + shifts * amplitudes.astype(jnp.float32)).astype(jnp.bflo...]
    unnamed x4 -> x6, local copies, waits for them, and re-layouts: 13.3 us -> 3.55 us
  transfers between devices with their start and end apart: 4 -> 2, of which waited for: 4 -> 2; matrix products, arithmetic and copies ran while one was open for 14% -> 2% of each run, Pallas kernels for 7% -> 0%
where the time goes in v1:
time: 236 us; the launch traced here: 232 us
  blocking collectives  83.9 us (36%)
  waiting for transfers between devices  76.4 us (32%)
  Pallas kernels  51.4 us (22%)
  local copies, waits for them, and re-layouts  10.5 us (4%)
  starting transfers between devices  9.74 us (4%)
    all_to_all x1, blocking collectives, by_slabs(): crossing = lax.all_to_all(crossing, ('aa', 'ba', 'col'), 0, 0, tiled=True)  83.9 us
    all_to_all x1, waiting for transfers between devices, by_slabs(): lax.all_to_all(total.reshape(peers, share * rows, LANES), ('aa', 'col'),...  38.3 us
    all_to_all x1, waiting for transfers between devices, by_slabs(): lax.all_to_all(packed, ('aa', 'col'), 0, 0, tiled=True)  38.1 us
    pallas_call x1, Pallas kernels, ladders_of_slabs(): pl.pallas_call(functools.partial(ladder_kernel, sizes), grid=(share // co...  20.1 us
    pallas_call x1, Pallas kernels, joined(): pl.pallas_call(functools.partial(joining_kernel, sizes), grid=(1,), in_sp...  12.5 us
    pallas_call x1, Pallas kernels, closed(): pl.pallas_call(closing_kernel, grid=(width_b // group,), in_specs=[pl.Blo...  10.5 us
    pallas_call x1, Pallas kernels, pack(): pl.pallas_call(functools.partial(pack_kernel, rows), grid=(width_b // gro...  8.24 us
    all_to_all x1, starting transfers between devices, by_slabs(): lax.all_to_all(total.reshape(peers, share * rows, LANES), ('aa', 'col'),...  5.21 us
  transfers between devices with their start and end apart: 2, of which 2 were waited for; matrix products, arithmetic and copies ran while one was open for 2% of the time, Pallas kernels for 0%

profile of v1, /device:TPU:11, one launch (start us, length us, event | category | flops | bytes accessed | tf_op | source)
XLA Modules:
  0.0 232.0 jit_solution(4687773533920545958)
XLA Ops:
  0.0 8.2 %shard_map.37 = bf16[96,144,128]{2,1,0:T(8,128)(2,1)} custom-call(bf16[192,96,96]{2,1,0:T(8,128)(2,1)} %amplitudes_ref.3), custom_call_target="tpu_custom_call" | custom-call | tf_op jit(solution)/shard_map/pallas_call | solution.py:91
  8.2 4.5 %all-to-all-start = ((bf16[8,1728,128]{2,1,0:T(8,128)(2,1)}), bf16[8,1728,128]{2,1,0:T(8,128)(2,1)S(1)}, u32[]{:S(2)}, u32[]{:S(2)}) async-start(bf16[8,1728,128]{2,1,0:T(8,128)(2,1)} %bitcast.18), calls=%async_computation | async-start | bytes 7077888 | tf_op jit(solution)/shard_map/all_to_all | solution.py:245
  12.8 2.4 %copy.7 = bf16[4,384,384]{2,1,0:T(8,128)(2,1)} copy(bf16[4,384,384]{1,2,0:T(8,128)(2,1)} %bitcast.22) | data formatting | bytes 2359296 | tf_op jit(solution)/shard_map/transpose | solution.py:240
  15.2 38.1 %all-to-all-done = bf16[8,1728,128]{2,1,0:T(8,128)(2,1)S(1)} async-done(((bf16[8,1728,128]{2,1,0:T(8,128)(2,1)}), bf16[8,1728,128]{2,1,0:T(8,128)(2,1)S(1)}, u32[]{:S(2)}, u32[]{:S(2)}) %all-to-all-start) | async-done | bytes 3538976 | tf_op jit(solution)/shard_map/all_to_all | solution.py:245
  53.3 0.0 copy-start.1
  53.3 1.8 copy-done.1
  55.1 20.1 %shard_map.38 = (bf16[12,384,384]{2,1,0:T(8,128)(2,1)}, bf16[32,144,384]{2,1,0:T(8,128)(2,1)}) custom-call(bf16[8,12,144,128]{3,2,1,0:T(8,128)(2,1)} %bitcast.20, bf16[1536,384]{1,0:T(8,128)(2,1)} %bitcast.23, bf16[1536,384]{1,0:T(8,128)(2,1)} %bitcast.24), custom_call_target="tpu_custom_call" | custom-call | flops 10871635968 | bytes 14155776 | tf_op jit(solution)/shard_map/pallas_call | solution.py:133
  75.2 2.4 %copy.8 = bf16[4,2,4,144,384]{4,3,2,0,1:T(8,128)(2,1)S(1)} copy(bf16[4,2,4,144,384]{4,3,2,1,0:T(8,128)(2,1)} %bitcast.21) | data formatting | bytes 7077888 | tf_op jit(solution)/shard_map/reshape | solution.py:247
  77.6 83.9 %all_to_all.15.rows_ref = bf16[32,144,384]{2,1,0:T(8,128)(2,1)} all-to-all(bf16[32,144,384]{2,1,0:T(8,128)(2,1)S(1)} %bitcast.17), channel_id=1, replica_groups=mesh['aa'=2,'ba'=4,'col'=4] {'aa','ba','col'}, dimensions={0} | all-to-all | bytes 7077888 | tf_op jit(solution)/shard_map/all_to_all | solution.py:249
  161.5 12.5 %shard_map.39 = bf16[8,12,144,128]{3,2,1,0:T(8,128)(2,1)} custom-call(bf16[12,384,384]{2,1,0:T(8,128)(2,1)} %get-tuple-element.7.ladder_ref, bf16[32,144,384]{2,1,0:T(8,128)(2,1)} %all_to_all.15.rows_ref), custom_call_target="tpu_custom_call" | custom-call | tf_op jit(solution)/shard_map/pallas_call | solution.py:188
  174.0 0.0 copy-start.2
  174.0 5.2 %all-to-all-start.2 = ((bf16[8,1728,128]{2,1,0:T(8,128)(2,1)}), bf16[8,1728,128]{2,1,0:T(8,128)(2,1)S(1)}, u32[]{:S(2)}, u32[]{:S(2)}) async-start(bf16[8,1728,128]{2,1,0:T(8,128)(2,1)} %bitcast.19), calls=%async_computation.2 | async-start | bytes 7077888 | tf_op jit(solution)/shard_map/all_to_all | solution.py:251
  179.3 0.0 copy-done.2
  179.3 0.1 dynamic_slice.9
  179.3 0.8 copy.9.shift_a_ref
  180.1 0.7 dynamic-slice_bitcast_fusion
  180.8 0.7 copy.10.shift_b_ref
  181.5 38.3 %all-to-all-done.2 = bf16[8,1728,128]{2,1,0:T(8,128)(2,1)S(1)} async-done(((bf16[8,1728,128]{2,1,0:T(8,128)(2,1)}), bf16[8,1728,128]{2,1,0:T(8,128)(2,1)S(1)}, u32[]{:S(2)}, u32[]{:S(2)}) %all-to-all-start.2) | async-done | bytes 3538976 | tf_op jit(solution)/shard_map/all_to_all | solution.py:251
  219.8 0.0 copy-start
  219.8 1.8 copy-done
  221.5 10.5 %shard_map.40 = bf16[192,96,96]{2,1,0:T(8,128)(2,1)} custom-call(bf16[96,144,128]{2,1,0:T(8,128)(2,1)} %bitcast.16, bf16[192,96,96]{2,1,0:T(8,128)(2,1)} %amplitudes_ref.3, f32[192,1,1]{2,1,0:T(1,128)} %copy.9.shift_a_ref, f32[1,96,1]{2,1,0:T(8,128)} %copy.10.shift_b_ref, f32[1,1,96]{2,1,0:T(1,128)} %get-tuple-element.9.shift_c_ref), custom_call_target="tpu_custom_call" | custom-call | tf_op jit(solution)/shard_map/pallas_call | solution.py:216
Async XLA Ops:
  8.2 45.0 %all-to-all-start = ((bf16[8,1728,128]{2,1,0:T(8,128)(2,1)}), bf16[8,1728,128]{2,1,0:T(8,128)(2,1)S(1)}, u32[]{:S(2)}, u32[]{:S(2)}) async-start(bf16[8,1728,128]{2,1,0:T(8,128)(2,1)} %bitcast.18), calls=%async_computation | async-start | bytes 7077888 | tf_op jit(solution)/shard_map/all_to_all | solution.py:245
  53.3 1.8 copy-start.1
  174.0 5.2 %copy-start.2 = (f32[384]{0:T(512)S(1)}, f32[384]{0:T(512)}, u32[]{:S(2)}) copy-start(f32[384]{0:T(512)} %param.5) | copy-start | bytes 4612
  174.0 45.7 %all-to-all-start.2 = ((bf16[8,1728,128]{2,1,0:T(8,128)(2,1)}), bf16[8,1728,128]{2,1,0:T(8,128)(2,1)S(1)}, u32[]{:S(2)}, u32[]{:S(2)}) async-start(bf16[8,1728,128]{2,1,0:T(8,128)(2,1)} %bitcast.19), calls=%async_computation.2 | async-start | bytes 7077888 | tf_op jit(solution)/shard_map/all_to_all | solution.py:251
  219.8 1.8 copy-start
